TPU v7x, 32 devices: a whole 2x2x4 slice. The times are simulated.
32 devices in a mesh: dp: 8 (over z, y), expert: 4 (over x, core).
Axes of the slice: x: 2, y: 2, z: 4, core: 2. Of those that a mesh axis runs over, the one named last changes fastest.
Arguments:
- queries: bfloat16 [4096, 4096], P('dp', 'expert'), may hold values from -6 to 6
- key_states: bfloat16 [4096, 4096], P('dp', 'expert'), may hold values from -6 to 6
- value_states: bfloat16 [4096, 4096], P('dp', 'expert'), may hold values from -6 to 6
- doc_lengths: int32 [8, 8], replicated, may hold values from 0 to 512, as said below
- move_plan: int32 [8, 2], replicated, may hold values from 0 to 7, as said below
- expert_ids: int32 [4096, 8], P('dp'), may hold values from 0 to 15, all different within a row; in each aligned block of 512 rows (0 to 511, 512 to 1023, ...) at most 384 rows name the same one
- gate_weights: float32 [4096, 8], P('dp'), may hold values from 0.05 to 0.5
- expert_weight: bfloat16 [16, 4096, 1024], P('expert'), may hold values from -0.29882812 to 0.29882812
Outputs:
- attended: bfloat16 [4096, 4096], P('dp', 'expert')
- combined: bfloat16 [4096, 1024], P('dp', 'expert')
- row_load: float32 [8], P('dp')
Inputs may be any that keep to these rules, and one draw needn't show every extreme that they name: `doc_lengths`: each row's entries are the lengths of its packed documents in order and sum to 512; a zero marks an absent document; some row holds a single document. move_plan[r, 0] is r itself or the row half the dp axis away, (r + 8 / 2) mod 8; a row is handed to its partner only if its pairs in all exceed the partner's, so two partners never both move; move_plan[r, 1] is a block number below 2; at least one row moves a block. `expert_ids`: each token names 8 different experts; among the 512 tokens of one row no expert is named by more than 384 tokens.
All inputs are finite; a program needn't handle non-finite values.
Results may differ from a plain program's by a relative error of at most 0.0095.
Values may be sent and summed in bfloat16 or wider, within the bound.
A program may use at most 128 MiB of HBM per device.

v0:
```python
import jax
import jax.numpy as jnp
from jax import lax
from jax.sharding import PartitionSpec as P

HEAD_DIM = 128
QBLOCK = 128
BLOCKS = 4
EXPERTS = 16
CAP = 384


def token_starts(row_lengths, row_count):
    bounds = jnp.cumsum(row_lengths)
    positions = jnp.arange(row_count, dtype=jnp.int32)
    return jnp.max(jnp.where(bounds[None, :] <= positions[:, None], bounds[None, :], 0), axis=1)


def block_pairs(row_lengths, row_count):
    positions = jnp.arange(row_count, dtype=jnp.int32)
    reach = positions - token_starts(row_lengths, row_count) + 1
    return reach.reshape(BLOCKS, QBLOCK).sum(axis=1)


def attend(query_rows, key_rows, value_rows, query_positions, query_starts):
    query_count = query_rows.shape[0]
    key_count = key_rows.shape[0]
    head_count = query_rows.shape[1] // HEAD_DIM
    query_heads = query_rows.reshape(query_count, head_count, HEAD_DIM)
    key_heads = key_rows.reshape(key_count, head_count, HEAD_DIM)
    value_heads = value_rows.reshape(key_count, head_count, HEAD_DIM)
    scores = jnp.einsum(
        "qhd,khd->hqk", query_heads, key_heads, preferred_element_type=jnp.float32
    ) * HEAD_DIM ** (-0.5)
    key_positions = jnp.arange(key_count, dtype=jnp.int32)
    allowed = (key_positions[None, :] <= query_positions[:, None]) & (
        key_positions[None, :] >= query_starts[:, None]
    )
    scores = jnp.where(allowed[None], scores, -jnp.inf)
    weights = jax.nn.softmax(scores, axis=-1).astype(jnp.bfloat16)
    output = jnp.einsum("hqk,khd->qhd", weights, value_heads, preferred_element_type=jnp.float32)
    return output.reshape(query_count, head_count * HEAD_DIM).astype(jnp.bfloat16)


def shards(
    queries,
    key_states,
    value_states,
    doc_lengths,
    move_plan,
    expert_ids,
    gate_weights,
    expert_weight,
):
    dp_size = lax.axis_size("dp")
    group_size = lax.axis_size("expert")
    own_row = lax.axis_index("dp")
    partner = (own_row + dp_size // 2) % dp_size
    row_count = queries.shape[0]
    positions = jnp.arange(row_count, dtype=jnp.int32)
    own_lengths = lax.dynamic_index_in_dim(doc_lengths, own_row, 0, keepdims=False)
    partner_lengths = lax.dynamic_index_in_dim(doc_lengths, partner, 0, keepdims=False)
    own_starts = token_starts(own_lengths, row_count)
    own_plan = lax.dynamic_index_in_dim(move_plan, own_row, 0, keepdims=False)
    partner_plan = lax.dynamic_index_in_dim(move_plan, partner, 0, keepdims=False)
    moving = own_plan[0] != own_row
    incoming = partner_plan[0] != partner
    own_block = own_plan[1]
    their_block = partner_plan[1]

    def run_block(block_index):
        low_row = block_index * QBLOCK
        high_row = low_row + QBLOCK
        return attend(
            queries[low_row:high_row],
            key_states[:high_row],
            value_states[:high_row],
            positions[low_row:high_row],
            own_starts[low_row:high_row],
        )

    attended = jnp.concatenate([run_block(block_index) for block_index in range(BLOCKS)], 0)
    own_pairs = block_pairs(own_lengths, row_count)
    partner_pairs = block_pairs(partner_lengths, row_count)
    row_work = (
        jnp.sum(own_pairs)
        - jnp.where(moving, own_pairs[own_block], 0)
        + jnp.where(incoming, partner_pairs[their_block], 0)
    )
    row_load = (row_work.astype(jnp.float32) / (QBLOCK * QBLOCK)).reshape(1)
    local_experts = EXPERTS // group_size
    expert_range = jnp.arange(EXPERTS, dtype=jnp.int32)
    matches = expert_ids[:, :, None] == expert_range[None, None, :]
    member = jnp.any(matches, axis=1)
    gate_table = jnp.sum(jnp.where(matches, gate_weights[:, :, None], 0.0), axis=1)
    earlier = (positions[None, :] < positions[:, None]).astype(jnp.bfloat16)
    slot_counts = jnp.dot(earlier, member.astype(jnp.bfloat16), preferred_element_type=jnp.float32)
    slot_of = slot_counts.astype(jnp.int32)
    slot_range = jnp.arange(CAP, dtype=jnp.int32)
    dispatch_hot = member.T[:, None, :] & (slot_of.T[:, None, :] == slot_range[None, :, None])
    filled = jnp.any(dispatch_hot, axis=2)
    source = jnp.sum(jnp.where(dispatch_hot, positions[None, None, :], 0), axis=2) + jnp.where(
        filled, 0, row_count
    )
    source = source.reshape(-1)
    member_index = lax.axis_index("expert")
    chosen_rows = lax.dynamic_slice_in_dim(
        source, member_index * local_experts * CAP, local_experts * CAP, 0
    )
    piece = lax.all_gather(attended, "expert", axis=1, tiled=True)
    extended = jnp.concatenate([piece, jnp.zeros((1, piece.shape[1]), piece.dtype)], 0)
    picked = extended[chosen_rows].reshape(local_experts, CAP, piece.shape[1])
    summed = jnp.einsum("ecf,efg->ecg", picked, expert_weight, preferred_element_type=jnp.float32)
    activated = jax.nn.silu(summed).astype(jnp.bfloat16)[None]
    spread = lax.all_to_all(activated, "expert", split_axis=3, concat_axis=0, tiled=True)
    outputs_table = spread.reshape(EXPERTS, CAP, spread.shape[3])
    selected = jnp.einsum(
        "ect,ecg->teg",
        dispatch_hot.astype(jnp.bfloat16),
        outputs_table,
        preferred_element_type=jnp.float32,
    )
    combined = jnp.sum(selected * gate_table[:, :, None], axis=1).astype(jnp.bfloat16)
    return (attended, combined, row_load)


def solution(mesh):
    in_specs = (
        P("dp", "expert"),
        P("dp", "expert"),
        P("dp", "expert"),
        P(),
        P(),
        P("dp", None),
        P("dp", None),
        P("expert", None, None),
    )
    out_specs = (P("dp", "expert"), P("dp", "expert"), P("dp"))
    return jax.shard_map(shards, mesh=mesh, in_specs=in_specs, out_specs=out_specs, check_vma=False)
```

profile of v0, /device:TPU:0, one launch (start us, length us, event | category | flops | bytes accessed | tf_op | source)
XLA Modules:
  0.0 178.1 jit_solution(11677466727423004778)
XLA Ops:
  7.2 0.8 fusion.53
  8.3 1.3 fusion.57
  9.8 0.4 copy.121
  10.3 1.6 multiply_select_fusion.2
  11.8 0.8 fusion.64
  13.1 0.3 fusion.19
  13.5 0.6 fusion.65
  14.1 0.6 copy-done
  14.7 1.3 copy.115
  16.0 1.2 copy.95
  17.2 4.2 %convolution_convert_fusion.2 = bf16[8,128,128]{1,2,0:T(8,128)(2,1)S(1)} fusion(bf16[384,8,128]{0,2,1:T(8,128)(2,1)} %bitcast.113, f32[8,128]{1,0:T(8,128)S(1)} %fusion.64, f32[8,128,384]{2,1,0:T(8,128)} %multiply_select_fusion.2), kind=kOutput, calls=%fused_computation.34 | convolution fusion | flops 101975424 | bytes 2625536 | tf_op jit(solution)/shard_map/hqk,khd->qhd/dot_general | solution.py:41
  21.4 0.9 copy.102
  22.5 1.9 %convolution_convert_fusion.3 = bf16[8,128,128]{1,2,0:T(8,128)(2,1)S(1)} fusion(bf16[256,8,128]{0,2,1:T(8,128)(2,1)S(1)} %bitcast.114, f32[8,128]{1,0:T(8,128)S(1)} %fusion.65, f32[8,128,256]{2,1,0:T(8,128)S(1)} %fusion.19), kind=kOutput, calls=%fused_computation.35 | convolution fusion | flops 68027648 | bytes 1839104 | tf_op jit(solution)/shard_map/hqk,khd->qhd/dot_general | solution.py:41
  26.4 2.3 %fusion.61 = (f32[8,128]{1,0:T(8,128)S(1)}, f32[8,128,512]{2,1,0:T(8,128)}) fusion(pred[128,512]{1,0:T(8,128)(4,1)S(1)} %fusion.32, bf16[128,8,128]{0,2,1:T(8,128)(2,1)S(1)} %bitcast.115, bf16[512,1024]{1,0:T(8,128)(2,1)S(1)} %copy-done.1), kind=kOutput, calls=%fused_computation.98 | convolution fusion | flops 136315392 | bytes 3477504 | tf_op jit(solution)/shard_map/sub | solution.py:40
  28.7 2.2 %convolution_convert_fusion = bf16[8,128,128]{1,2,0:T(8,128)(2,1)S(1)} fusion(bf16[512,8,128]{0,2,1:T(8,128)(2,1)S(1)} %bitcast.108, f32[8,128,512]{2,1,0:T(8,128)} %get-tuple-element.26, f32[8,128]{1,0:T(8,128)S(1)} %get-tuple-element.25), kind=kOutput, calls=%fused_computation.32 | convolution fusion | flops 135397376 | bytes 3411968 | tf_op jit(solution)/shard_map/hqk,khd->qhd/dot_general | solution.py:41
  31.1 1.0 pad_maximum_fusion
  32.4 2.1 %fusion.7 = pred[16,384]{1,0:T(8,128)(4,1)S(1)} fusion(s32[16,512]{1,0:T(8,128)S(1)} %convolution_convert_fusion.4, pred[16,512]{1,0:T(8,128)(4,1)S(1)} %bitcast.121), kind=kLoop, calls=%fused_computation.9 | loop fusion | flops 9431040 | bytes 47104 | tf_op jit(solution)/shard_map/reduce_or | solution.py:101
  34.5 2.8 %select_reduce_fusion = s32[16,384]{1,0:T(8,128)S(1)} fusion(s32[16,512]{1,0:T(8,128)S(1)} %convolution_convert_fusion.4, pred[16,512]{1,0:T(8,128)(4,1)S(1)} %bitcast.122), kind=kLoop, calls=%fused_computation.5 | loop fusion | flops 12576768 | bytes 65536 | tf_op jit(solution)/shard_map/reduce_sum | solution.py:102
  37.4 32.1 %all-gather.2.cloned.1.call-done = bf16[512,4096]{1,0:T(8,128)(2,1)} async-done(((bf16[512,1024]{1,0:T(8,128)(2,1)}), bf16[512,4096]{1,0:T(8,128)(2,1)}) %all-gather.2.cloned.1.call-update) | async-done | bytes 4194320 | tf_op jit(solution)/shard_map/all_gather | solution.py:110
  69.5 4.7 %concatenate.7 = bf16[513,4096]{1,0:T(8,128)(2,1)} pad(bf16[512,4096]{1,0:T(8,128)(2,1)} %all-gather.2.cloned.1.call-done, bf16[]{:T(256)} %constant.66.clone.1), padding=0_1x0_0 | pad | bytes 8396802 | tf_op jit(solution)/shard_map/concatenate | solution.py:111
  74.2 25.0 %gather_fusion = bf16[1536,4096]{1,0:T(8,128)(2,1)} fusion(bf16[513,4096]{1,0:T(8,128)(2,1)} %concatenate.7, s32[2048]{0:T(1024)S(1)} %pad_clamp_fusion), kind=kCustom, calls=%fused_computation | custom fusion | bytes 25171968 | tf_op jit(solution)/shard_map/gather | solution.py:112
  99.2 21.3 %fusion.11 = bf16[1,4,384,1024]{3,2,1,0:T(8,128)(2,1)S(1)} fusion(bf16[4,384,4096]{2,1,0:T(8,128)(2,1)} %bitcast.99, bf16[4,4096,1024]{2,1,0:T(8,128)(2,1)} %param.15), kind=kOutput, calls=%fused_computation.15 | convolution fusion | flops 12892766208 | bytes 49283072 | tf_op jit(solution)/shard_map/ecf,efg->ecg/dot_general | solution.py:113
  120.5 3.8 %copy.104 = bf16[1,4,384,1024]{2,1,0,3:T(4,128)(2,1)} copy(bf16[1,4,384,1024]{3,2,1,0:T(8,128)(2,1)S(1)} %fusion.11) | data formatting | bytes 6291456 | tf_op jit(solution)/shard_map/broadcast_in_dim | solution.py:114
  124.3 4.1 %all-to-all-start = ((bf16[1,4,384,1024]{2,1,0,3:T(4,128)(2,1)}), bf16[1,4,384,1024]{2,1,0,3:T(4,128)(2,1)S(1)}, u32[]{:S(2)}, u32[]{:S(2)}) async-start(bf16[1,4,384,1024]{2,1,0,3:T(4,128)(2,1)} %copy.104), calls=%async_computation | async-start | bytes 6291456 | tf_op jit(solution)/shard_map/all_to_all | solution.py:115
  128.5 0.5 fusion.59
  133.7 0.6 dynamic_slice.26
  134.9 0.6 add_reduce_fusion
  137.0 0.6 dynamic_slice.29
  138.3 26.6 %all-to-all-done = bf16[1,4,384,1024]{2,1,0,3:T(4,128)(2,1)S(1)} async-done(((bf16[1,4,384,1024]{2,1,0,3:T(4,128)(2,1)}), bf16[1,4,384,1024]{2,1,0,3:T(4,128)(2,1)S(1)}, u32[]{:S(2)}, u32[]{:S(2)}) %all-to-all-start) | async-done | bytes 3145760 | tf_op jit(solution)/shard_map/all_to_all | solution.py:115
  165.0 0.6 copy.105
  165.5 3.8 %fusion.8 = bf16[512,256]{0,1:T(8,128)(2,1)S(1)} fusion(f32[512,16]{0,1:T(8,128)S(1)} %select_reduce_fusion.1, bf16[16,384,256]{1,2,0:T(8,128)(2,1)S(1)} %bitcast.101, s32[16,512]{1,0:T(8,128)S(1)} %convolution_convert_fusion.4, pred[16,512]{1,0:T(8,128)(4,1)S(1)} %bitcast.123), kind=kOutput, calls=%fused_computation.11 | convolution fusion | flops 1620967424 | bytes 3481600 | tf_op jit(solution)/shard_map/ect,ecg->teg/dot_general | solution.py:117
  169.3 0.8 copy.106
  (68 shorter events, 4.3 us)
Async XLA Ops:
  7.2 2.6 %slice-start.3 = ((bf16[512,1024]{1,0:T(8,128)(2,1)}), bf16[384,1024]{1,0:T(8,128)(2,1)S(1)}, s32[]{:S(2)}) async-start(bf16[512,1024]{1,0:T(8,128)(2,1)} %param.9), calls=%async_computation.5 | async-start | bytes 1572864 | tf_op jit(solution)/shard_map/slice | solution.py:76
  7.2 62.3 %all-gather.2.cloned.1.call-start = ((), (), s32[]{:S(2)}) async-start(), calls=%async_computation.1 | async-start | bytes 5242880 | tf_op jit(solution)/shard_map/all_gather | solution.py:110
  10.2 2.5 %slice-start.4 = ((bf16[512,1024]{1,0:T(8,128)(2,1)}), bf16[256,1024]{1,0:T(8,128)(2,1)S(1)}, s32[]{:S(2)}) async-start(bf16[512,1024]{1,0:T(8,128)(2,1)} %param.9), calls=%async_computation.6 | async-start | bytes 1048576 | tf_op jit(solution)/shard_map/slice | solution.py:76
  13.5 1.2 copy-start
  14.1 1.9 %slice-start = ((bf16[512,1024]{1,0:T(8,128)(2,1)}), bf16[384,1024]{1,0:T(8,128)(2,1)S(1)}, s32[]{:S(2)}) async-start(bf16[512,1024]{1,0:T(8,128)(2,1)} %param.10), calls=%async_computation.2 | async-start | bytes 1572864 | tf_op jit(solution)/shard_map/slice | solution.py:77
  17.2 5.0 %slice-start.1 = ((bf16[512,1024]{1,0:T(8,128)(2,1)}), bf16[256,1024]{1,0:T(8,128)(2,1)S(1)}, s32[]{:S(2)}) async-start(bf16[512,1024]{1,0:T(8,128)(2,1)} %param.10), calls=%async_computation.3 | async-start | bytes 1048576 | tf_op jit(solution)/shard_map/slice | solution.py:77
  22.4 2.3 %slice-start.5 = ((bf16[512,1024]{1,0:T(8,128)(2,1)}), bf16[128,1024]{1,0:T(8,128)(2,1)S(1)}, s32[]{:S(2)}) async-start(bf16[512,1024]{1,0:T(8,128)(2,1)} %param.9), calls=%async_computation.7 | async-start | bytes 524288 | tf_op jit(solution)/shard_map/slice | solution.py:76
  22.4 3.0 %slice-start.2 = ((bf16[512,1024]{1,0:T(8,128)(2,1)}), bf16[128,1024]{1,0:T(8,128)(2,1)S(1)}, s32[]{:S(2)}) async-start(bf16[512,1024]{1,0:T(8,128)(2,1)} %param.10), calls=%async_computation.4 | async-start | bytes 524288 | tf_op jit(solution)/shard_map/slice | solution.py:77
  24.8 1.6 copy-start.1
  25.9 2.8 %copy-start.2 = (bf16[512,1024]{0,1:T(8,128)(2,1)S(1)}, bf16[512,1024]{0,1:T(8,128)(2,1)}, u32[]{:S(2)}) copy-start(bf16[512,1024]{0,1:T(8,128)(2,1)} %copy.115) | copy-start | bytes 3145732
  28.7 2.3 %copy-start.3 = (bf16[128,1024]{1,0:T(8,128)(2,1)S(1)}, bf16[128,1024]{1,0:T(8,128)(2,1)}, u32[]{:S(2)}) copy-start(bf16[128,1024]{1,0:T(8,128)(2,1)} %copy.102) | copy-start | bytes 786436
  30.9 1.2 copy-start.4
  124.3 4.1 %copy-start.6 = (s32[8,2]{0,1:T(2,128)S(1)}, s32[8,2]{0,1:T(2,128)}, u32[]{:S(2)}) copy-start(s32[8,2]{0,1:T(2,128)} %param.12) | copy-start | bytes 196
  124.3 14.0 %copy-start.5 = (f32[512,8]{0,1:T(8,128)S(1)}, f32[512,8]{0,1:T(8,128)}, u32[]{:S(2)}) copy-start(f32[512,8]{0,1:T(8,128)} %param.14) | copy-start | bytes 49156
  124.3 40.7 %all-to-all-start = ((bf16[1,4,384,1024]{2,1,0,3:T(4,128)(2,1)}), bf16[1,4,384,1024]{2,1,0,3:T(4,128)(2,1)S(1)}, u32[]{:S(2)}, u32[]{:S(2)}) async-start(bf16[1,4,384,1024]{2,1,0,3:T(4,128)(2,1)} %copy.104), calls=%async_computation | async-start | bytes 6291456 | tf_op jit(solution)/shard_map/all_to_all | solution.py:115
Sparse Core Ops, SparseCore 0:
  32.2 37.1 all-gather.1
where the time goes:
time: 179 us; the launch traced here: 178 us
  waiting for transfers between devices  58.7 us (33%)
  local copies, waits for them, and re-layouts  44.9 us (25%)
  matrix products  39.8 us (22%)
  between operations  22.6 us (13%)
  other arithmetic  7.99 us (4%)
  starting transfers between devices  4.13 us (2%)
    all_gather x1, waiting for transfers between devices, shards(): piece = lax.all_gather(attended, 'expert', axis=1, tiled=True)  32.1 us
    all_to_all x1, waiting for transfers between devices, shards(): lax.all_to_all(activated, 'expert', split_axis=3, concat_axis=0, tiled=True)  26.6 us
    gather x1, local copies, waits for them, and re-layouts, shards(): picked = extended[chosen_rows].reshape(local_experts, CAP, piece.shape[1])  25 us
    dot_general x1, matrix products, shards(): jnp.einsum('ecf,efg->ecg', picked, expert_weight, preferred_element_type=...  21.3 us
    dot_general x4, matrix products, attend(): jnp.einsum('hqk,khd->qhd', weights, value_heads, preferred_element_type=j...  8.57 us
    concatenate x1, local copies, waits for them, and re-layouts, shards(): jnp.concatenate([piece, jnp.zeros((1, piece.shape[1]), piece.dtype)], 0)  4.7 us
    all_to_all x1, starting transfers between devices, shards(): lax.all_to_all(activated, 'expert', split_axis=3, concat_axis=0, tiled=True)  4.09 us
    broadcast_in_dim x1, local copies, waits for them, and re-layouts, shards(): activated = jax.nn.silu(summed).astype(jnp.bfloat16)[None]  3.76 us
  transfers between devices with their start and end apart: 2, of which 2 were waited for; matrix products, arithmetic and copies ran while one was open for 5% of the time, Pallas kernels for 0%

commit v1 on v0

--- a/solution.py
+++ b/solution.py
@@ -107,7 +107,7 @@
     chosen_rows = lax.dynamic_slice_in_dim(
         source, member_index * local_experts * CAP, local_experts * CAP, 0
     )
-    piece = lax.all_gather(attended, "expert", axis=1, tiled=True)
+    piece = jnp.concatenate(lax.all_gather(attended, "expert"), axis=1)
     extended = jnp.concatenate([piece, jnp.zeros((1, piece.shape[1]), piece.dtype)], 0)
     picked = extended[chosen_rows].reshape(local_experts, CAP, piece.shape[1])
     summed = jnp.einsum("ecf,efg->ecg", picked, expert_weight, preferred_element_type=jnp.float32)

time: 179 us -> 184 us (1.028)
  local copies, waits for them, and re-layouts: 44.9 us -> 50.4 us
    all_gather x0 -> x1, local copies, waits for them, and re-layouts: none -> 5.64 us  [shards(): piece = jnp.concatenate(lax.all_gather(attended, 'expert'), axis=1)]
    unnamed x22 -> x23, local copies, waits for them, and re-layouts: 2.83 us -> 5.16 us
    concatenate x1, local copies, waits for them, and re-layouts: 4.7 us -> 2.46 us  [shards(): jnp.concatenate([piece, jnp.zeros((1, piece.shape[1]), piece.dtype)], 0)]
  transfers between devices with their start and end apart: 2 -> 2, of which waited for: 2 -> 2; matrix products, arithmetic and copies ran while one was open for 5% -> 4% of each run, Pallas kernels for 0% -> 0%
where the time goes in v1:
time: 184 us
  waiting for transfers between devices  59 us (32%)
  local copies, waits for them, and re-layouts  50.4 us (27%)
  matrix products  39.8 us (22%)
  between operations  22.6 us (12%)
  other arithmetic  7.99 us (4%)
  starting transfers between devices  3.87 us (2%)
    all_gather x1, waiting for transfers between devices, shards(): piece = jnp.concatenate(lax.all_gather(attended, 'expert'), axis=1)  32.1 us
    all_to_all x1, waiting for transfers between devices, shards(): lax.all_to_all(activated, 'expert', split_axis=3, concat_axis=0, tiled=True)  26.9 us
    gather x1, local copies, waits for them, and re-layouts, shards(): picked = extended[chosen_rows].reshape(local_experts, CAP, piece.shape[1])  24.8 us
    dot_general x1, matrix products, shards(): jnp.einsum('ecf,efg->ecg', picked, expert_weight, preferred_element_type=...  21.3 us
    dot_general x4, matrix products, attend(): jnp.einsum('hqk,khd->qhd', weights, value_heads, preferred_element_type=j...  8.57 us
    all_gather x1, local copies, waits for them, and re-layouts, shards(): piece = jnp.concatenate(lax.all_gather(attended, 'expert'), axis=1)  5.64 us
    unnamed x23, local copies, waits for them, and re-layouts  5.16 us
    all_to_all x1, starting transfers between devices, shards(): lax.all_to_all(activated, 'expert', split_axis=3, concat_axis=0, tiled=True)  3.83 us
  transfers between devices with their start and end apart: 2, of which 2 were waited for; matrix products, arithmetic and copies ran while one was open for 4% of the time, Pallas kernels for 0%

profile of v1, /device:TPU:0, one launch (start us, length us, event | category | flops | bytes accessed | tf_op | source)
XLA Modules:
  0.0 183.7 jit_solution(2634738350947091797)
XLA Ops:
  7.2 0.8 fusion.53
  8.3 1.3 fusion.57
  10.3 1.6 multiply_select_fusion.2
  11.8 0.8 fusion.64
  13.5 0.6 fusion.65
  14.1 0.6 copy-done
  14.7 1.3 copy.119
  16.0 1.2 copy.98
  17.2 4.2 %convolution_convert_fusion.2 = bf16[8,128,128]{1,2,0:T(8,128)(2,1)S(1)} fusion(bf16[384,8,128]{0,2,1:T(8,128)(2,1)} %bitcast.120, f32[8,128]{1,0:T(8,128)S(1)} %fusion.64, f32[8,128,384]{2,1,0:T(8,128)} %multiply_select_fusion.2), kind=kOutput, calls=%fused_computation.34 | convolution fusion | flops 101975424 | bytes 2625536 | tf_op jit(solution)/shard_map/hqk,khd->qhd/dot_general | solution.py:41
  21.4 0.9 copy.105
  22.5 1.9 %convolution_convert_fusion.3 = bf16[8,128,128]{1,2,0:T(8,128)(2,1)S(1)} fusion(bf16[256,8,128]{0,2,1:T(8,128)(2,1)S(1)} %bitcast.121, f32[8,128]{1,0:T(8,128)S(1)} %fusion.65, f32[8,128,256]{2,1,0:T(8,128)S(1)} %fusion.19), kind=kOutput, calls=%fused_computation.35 | convolution fusion | flops 68027648 | bytes 1839104 | tf_op jit(solution)/shard_map/hqk,khd->qhd/dot_general | solution.py:41
  26.4 2.3 %fusion.61 = (f32[8,128]{1,0:T(8,128)S(1)}, f32[8,128,512]{2,1,0:T(8,128)}) fusion(pred[128,512]{1,0:T(8,128)(4,1)S(1)} %fusion.32, bf16[128,8,128]{0,2,1:T(8,128)(2,1)S(1)} %bitcast.122, bf16[512,1024]{1,0:T(8,128)(2,1)S(1)} %copy-done.1), kind=kOutput, calls=%fused_computation.98 | convolution fusion | flops 136315392 | bytes 3477504 | tf_op jit(solution)/shard_map/sub | solution.py:40
  28.7 2.2 %convolution_convert_fusion = bf16[8,128,128]{1,2,0:T(8,128)(2,1)S(1)} fusion(bf16[512,8,128]{0,2,1:T(8,128)(2,1)S(1)} %bitcast.115, f32[8,128,512]{2,1,0:T(8,128)} %get-tuple-element.26, f32[8,128]{1,0:T(8,128)S(1)} %get-tuple-element.25), kind=kOutput, calls=%fused_computation.32 | convolution fusion | flops 135397376 | bytes 3411968 | tf_op jit(solution)/shard_map/hqk,khd->qhd/dot_general | solution.py:41
  31.1 1.0 pad_maximum_fusion
  32.4 2.1 %fusion.7 = pred[16,384]{1,0:T(8,128)(4,1)S(1)} fusion(s32[16,512]{1,0:T(8,128)S(1)} %convolution_convert_fusion.4, pred[16,512]{1,0:T(8,128)(4,1)S(1)} %bitcast.128), kind=kLoop, calls=%fused_computation.9 | loop fusion | flops 9431040 | bytes 47104 | tf_op jit(solution)/shard_map/reduce_or | solution.py:101
  34.5 2.8 %select_reduce_fusion = s32[16,384]{1,0:T(8,128)S(1)} fusion(s32[16,512]{1,0:T(8,128)S(1)} %convolution_convert_fusion.4, pred[16,512]{1,0:T(8,128)(4,1)S(1)} %bitcast.129), kind=kLoop, calls=%fused_computation.5 | loop fusion | flops 12576768 | bytes 65536 | tf_op jit(solution)/shard_map/reduce_sum | solution.py:102
  37.4 32.1 %all-gather.3.cloned.1.call-done = bf16[2048,1024]{1,0:T(8,128)(2,1)} async-done(((bf16[512,1024]{1,0:T(8,128)(2,1)}), bf16[2048,1024]{1,0:T(8,128)(2,1)}) %all-gather.3.cloned.1.call-update) | async-done | bytes 4194320 | tf_op jit(solution)/shard_map/all_gather | solution.py:110
  69.5 5.6 %copy.107 = bf16[4,512,1024]{2,0,1:T(4,128)(2,1)S(1)} copy(bf16[4,512,1024]{2,1,0:T(8,128)(2,1)} %bitcast.107) | data formatting | bytes 8388608 | tf_op jit(solution)/shard_map/all_gather | solution.py:110
  75.1 2.3 %copy.128 = bf16[64,8,4,1024]{3,1,2,0:T(8,128)(2,1)S(1)} copy(bf16[64,8,4,1024]{3,2,1,0:T(4,128)(2,1)S(1)} %bitcast.104) | data formatting | bytes 8388608
  77.4 2.5 %concatenate.7 = bf16[513,4096]{1,0:T(8,128)(2,1)} pad(bf16[512,4096]{1,0:T(8,128)(2,1)S(1)} %bitcast.103, bf16[]{:T(256)} %constant.66.clone.1), padding=0_1x0_0 | pad | bytes 8396802 | tf_op jit(solution)/shard_map/concatenate | solution.py:111
  79.9 24.8 %gather_fusion = bf16[1536,4096]{1,0:T(8,128)(2,1)} fusion(bf16[513,4096]{1,0:T(8,128)(2,1)} %concatenate.7, s32[2048]{0:T(1024)S(1)} %pad_clamp_fusion), kind=kCustom, calls=%fused_computation | custom fusion | bytes 25171968 | tf_op jit(solution)/shard_map/gather | solution.py:112
  104.7 21.3 %fusion.11 = bf16[1,4,384,1024]{3,2,1,0:T(8,128)(2,1)S(1)} fusion(bf16[4,384,4096]{2,1,0:T(8,128)(2,1)} %bitcast.105, bf16[4,4096,1024]{2,1,0:T(8,128)(2,1)} %param.15), kind=kOutput, calls=%fused_computation.15 | convolution fusion | flops 12892766208 | bytes 49283072 | tf_op jit(solution)/shard_map/ecf,efg->ecg/dot_general | solution.py:113
  126.0 3.8 %copy.108 = bf16[1,4,384,1024]{2,1,0,3:T(4,128)(2,1)} copy(bf16[1,4,384,1024]{3,2,1,0:T(8,128)(2,1)S(1)} %fusion.11) | data formatting | bytes 6291456 | tf_op jit(solution)/shard_map/broadcast_in_dim | solution.py:114
  129.8 3.8 %all-to-all-start = ((bf16[1,4,384,1024]{2,1,0,3:T(4,128)(2,1)}), bf16[1,4,384,1024]{2,1,0,3:T(4,128)(2,1)S(1)}, u32[]{:S(2)}, u32[]{:S(2)}) async-start(bf16[1,4,384,1024]{2,1,0,3:T(4,128)(2,1)} %copy.108), calls=%async_computation | async-start | bytes 6291456 | tf_op jit(solution)/shard_map/all_to_all | solution.py:115
  133.7 0.5 fusion.59
  138.9 0.6 dynamic_slice.26
  140.1 0.6 add_reduce_fusion
  142.3 0.6 dynamic_slice.29
  143.6 26.9 %all-to-all-done = bf16[1,4,384,1024]{2,1,0,3:T(4,128)(2,1)S(1)} async-done(((bf16[1,4,384,1024]{2,1,0,3:T(4,128)(2,1)}), bf16[1,4,384,1024]{2,1,0,3:T(4,128)(2,1)S(1)}, u32[]{:S(2)}, u32[]{:S(2)}) %all-to-all-start) | async-done | bytes 3145760 | tf_op jit(solution)/shard_map/all_to_all | solution.py:115
  170.5 0.6 copy.109
  171.1 3.8 %fusion.8 = bf16[512,256]{0,1:T(8,128)(2,1)S(1)} fusion(f32[512,16]{0,1:T(8,128)S(1)} %select_reduce_fusion.1, bf16[16,384,256]{1,2,0:T(8,128)(2,1)S(1)} %bitcast.108, s32[16,512]{1,0:T(8,128)S(1)} %convolution_convert_fusion.4, pred[16,512]{1,0:T(8,128)(4,1)S(1)} %bitcast.130), kind=kOutput, calls=%fused_computation.11 | convolution fusion | flops 1620967424 | bytes 3481600 | tf_op jit(solution)/shard_map/ect,ecg->teg/dot_general | solution.py:117
  174.8 0.8 copy.110
  (70 shorter events, 5.0 us)
Async XLA Ops:
  7.2 2.6 %slice-start.3 = ((bf16[512,1024]{1,0:T(8,128)(2,1)}), bf16[384,1024]{1,0:T(8,128)(2,1)S(1)}, s32[]{:S(2)}) async-start(bf16[512,1024]{1,0:T(8,128)(2,1)} %param.9), calls=%async_computation.5 | async-start | bytes 1572864 | tf_op jit(solution)/shard_map/slice | solution.py:76
  7.2 62.3 %all-gather.3.cloned.1.call-start = ((), (), s32[]{:S(2)}) async-start(), calls=%async_computation.1 | async-start | bytes 5242880 | tf_op jit(solution)/shard_map/all_gather | solution.py:110
  10.2 2.5 %slice-start.4 = ((bf16[512,1024]{1,0:T(8,128)(2,1)}), bf16[256,1024]{1,0:T(8,128)(2,1)S(1)}, s32[]{:S(2)}) async-start(bf16[512,1024]{1,0:T(8,128)(2,1)} %param.9), calls=%async_computation.6 | async-start | bytes 1048576 | tf_op jit(solution)/shard_map/slice | solution.py:76
  13.5 1.2 copy-start
  14.1 1.9 %slice-start = ((bf16[512,1024]{1,0:T(8,128)(2,1)}), bf16[384,1024]{1,0:T(8,128)(2,1)S(1)}, s32[]{:S(2)}) async-start(bf16[512,1024]{1,0:T(8,128)(2,1)} %param.10), calls=%async_computation.2 | async-start | bytes 1572864 | tf_op jit(solution)/shard_map/slice | solution.py:77
  17.2 5.0 %slice-start.1 = ((bf16[512,1024]{1,0:T(8,128)(2,1)}), bf16[256,1024]{1,0:T(8,128)(2,1)S(1)}, s32[]{:S(2)}) async-start(bf16[512,1024]{1,0:T(8,128)(2,1)} %param.10), calls=%async_computation.3 | async-start | bytes 1048576 | tf_op jit(solution)/shard_map/slice | solution.py:77
  22.4 2.3 %slice-start.5 = ((bf16[512,1024]{1,0:T(8,128)(2,1)}), bf16[128,1024]{1,0:T(8,128)(2,1)S(1)}, s32[]{:S(2)}) async-start(bf16[512,1024]{1,0:T(8,128)(2,1)} %param.9), calls=%async_computation.7 | async-start | bytes 524288 | tf_op jit(solution)/shard_map/slice | solution.py:76
  22.4 3.0 %slice-start.2 = ((bf16[512,1024]{1,0:T(8,128)(2,1)}), bf16[128,1024]{1,0:T(8,128)(2,1)S(1)}, s32[]{:S(2)}) async-start(bf16[512,1024]{1,0:T(8,128)(2,1)} %param.10), calls=%async_computation.4 | async-start | bytes 524288 | tf_op jit(solution)/shard_map/slice | solution.py:77
  24.8 1.6 copy-start.1
  25.9 2.8 %copy-start.2 = (bf16[512,1024]{0,1:T(8,128)(2,1)S(1)}, bf16[512,1024]{0,1:T(8,128)(2,1)}, u32[]{:S(2)}) copy-start(bf16[512,1024]{0,1:T(8,128)(2,1)} %copy.119) | copy-start | bytes 3145732
  28.7 2.3 %copy-start.3 = (bf16[128,1024]{1,0:T(8,128)(2,1)S(1)}, bf16[128,1024]{1,0:T(8,128)(2,1)}, u32[]{:S(2)}) copy-start(bf16[128,1024]{1,0:T(8,128)(2,1)} %copy.105) | copy-start | bytes 786436
  30.9 1.2 copy-start.4
  129.8 3.8 %copy-start.6 = (s32[8,2]{0,1:T(2,128)S(1)}, s32[8,2]{0,1:T(2,128)}, u32[]{:S(2)}) copy-start(s32[8,2]{0,1:T(2,128)} %param.12) | copy-start | bytes 196
  129.8 13.8 %copy-start.5 = (f32[512,8]{0,1:T(8,128)S(1)}, f32[512,8]{0,1:T(8,128)}, u32[]{:S(2)}) copy-start(f32[512,8]{0,1:T(8,128)} %param.14) | copy-start | bytes 49156
  129.8 40.7 %all-to-all-start = ((bf16[1,4,384,1024]{2,1,0,3:T(4,128)(2,1)}), bf16[1,4,384,1024]{2,1,0,3:T(4,128)(2,1)S(1)}, u32[]{:S(2)}, u32[]{:S(2)}) async-start(bf16[1,4,384,1024]{2,1,0,3:T(4,128)(2,1)} %copy.108), calls=%async_computation | async-start | bytes 6291456 | tf_op jit(solution)/shard_map/all_to_all | solution.py:115
Sparse Core Ops, SparseCore 0:
  32.2 37.1 all-gather.2
